TPU v7x, 32 devices: a whole 2x2x4 slice. The times are simulated.
32 devices in a mesh: tenant: 2 (over y), ctx: 2 (over x), head: 8 (over z, core).
Axes of the slice: x: 2, y: 2, z: 4, core: 2. Of those that a mesh axis runs over, the one named last changes fastest.
Arguments:
- tokens: bfloat16 [1024, 4608], P(('tenant', 'ctx'), 'head'), parts along dimension 0, may hold values from -6 to 6
- query_frozen_matrix: bfloat16 [4608, 2048], P('ctx', 'head'), may hold values from -0.09375 to 0.09375
- key_weight: bfloat16 [4608, 1024], P('ctx', 'head'), may hold values from -0.09375 to 0.09375
- value_frozen_matrix: bfloat16 [4608, 1024], P('ctx', 'head'), may hold values from -0.09375 to 0.09375
- query_down: bfloat16 [9216, 16], P('tenant'), parts along dimension 0, may hold values from -0.09375 to 0.09375
- query_adapter_expand: bfloat16 [32, 2048], P('tenant', 'head'), parts along dimension 0, may hold values from -1.5 to 1.5
- value_down: bfloat16 [9216, 16], P('tenant'), parts along dimension 0, may hold values from -0.09375 to 0.09375
- value_adapter_expand: bfloat16 [32, 1024], P('tenant', 'head'), parts along dimension 0, may hold values from -1.5 to 1.5
- block_order: int32 [8], P('tenant'), parts along dimension 0, may hold values from 0 to 3, each once
- doc_starts: int32 [24], P('tenant'), parts along dimension 0, may hold values from 0 to 511, as said below
- prompt_of: int32 [24], P('tenant'), parts along dimension 0, may hold values from 0 to 11, as said below
Outputs:
- attended: bfloat16 [1024, 2048], P(('tenant', 'ctx'), 'head'), parts along dimension 0
There are 2 independent parts, one for each index of `tenant`. A program takes and returns all parts, laid end to end along the dimension named above; an argument that names none is the same for every part. Nothing has to cross between parts.
Inputs may be any that keep to these rules, and one draw needn't show every extreme that they name: `doc_starts`: strictly increasing with first entry 0; the segments come in 4 groups of three: a prompt, a chosen and a rejected response. `prompt_of`: for segment j = 3k it is j; for j = 3k + 1 it is 3k; for j = 3k + 2 it is 3k or j. `block_order`: each of 0 to 3 once.
All inputs are finite; a program needn't handle non-finite values.
Results may differ from a plain program's by a relative error of at most 0.012.
Values may be sent and summed in bfloat16 or wider, within the bound.
No kernel may reach another device: no remote copies, remote signals or barrier semaphores. Data moves between devices by JAX's collectives and lax.ppermute only.
A program may use at most 64 MiB of HBM per device.

v0:
```python
import math
import jax
import jax.numpy as jnp
from jax import lax
from jax.sharding import PartitionSpec as P

HD = 128
softcap_limit = 50.0
query_scale = 144.0 ** (-0.5)
adapter_scaling = 2.0
rope_base = 10000.0


def row_meta(row_ids, block_order, doc_starts, prompt_of, block_len, sequence_len):
    block_count = block_order.shape[0]
    block_id = row_ids // block_len
    one_hot = block_id[:, None] == jnp.arange(block_count, dtype=jnp.int32)[None, :]
    ordered = jnp.sum(jnp.where(one_hot, block_order[None, :], 0), axis=1)
    places = ordered * block_len + row_ids % block_len
    segment = jnp.sum((doc_starts[None, :] <= places[:, None]).astype(jnp.int32), axis=1) - 1
    seg_ids = jnp.arange(doc_starts.shape[0], dtype=jnp.int32)
    selected = segment[:, None] == seg_ids[None, :]
    prompt_seg = jnp.sum(jnp.where(selected, prompt_of[None, :], 0), axis=1)
    own_start = jnp.sum(jnp.where(selected, doc_starts[None, :], 0), axis=1)
    next_starts = jnp.concatenate([doc_starts[1:], jnp.full((1,), sequence_len, jnp.int32)])
    prompt_sel = prompt_seg[:, None] == seg_ids[None, :]
    prompt_len = jnp.sum(jnp.where(prompt_sel, (next_starts - doc_starts)[None, :], 0), axis=1)
    rotary_pos = places - own_start + jnp.where(prompt_seg != segment, prompt_len, 0)
    return (places, segment, prompt_seg, rotary_pos)


def rotate(values_in, rotary_pos):
    width_half = values_in.shape[-1] // 2
    frequency = jnp.exp(
        jnp.arange(width_half, dtype=jnp.float32)
        * (-2.0 * math.log(rope_base) / values_in.shape[-1])
    )
    angles = rotary_pos.astype(jnp.float32)[:, None] * frequency[None, :]
    cosine = jnp.concatenate([jnp.cos(angles), jnp.cos(angles)], axis=-1)[:, None, :]
    sine_part = jnp.concatenate([jnp.sin(angles), jnp.sin(angles)], axis=-1)[:, None, :]
    rotated = jnp.concatenate([-values_in[..., width_half:], values_in[..., :width_half]], axis=-1)
    return values_in * cosine + rotated * sine_part


def visible_mask(query_info, key_info):
    same_doc = (key_info[1][None, :] == query_info[1][:, None]) & (
        key_info[0][None, :] <= query_info[0][:, None]
    )
    from_prompt = (key_info[1][None, :] == query_info[2][:, None]) & (
        query_info[2] != query_info[1]
    )[:, None]
    return same_doc | from_prompt


def local(
    tokens,
    query_frozen_matrix,
    key_weight,
    value_frozen_matrix,
    query_down,
    query_adapter_expand,
    value_down,
    value_adapter_expand,
    block_order,
    doc_starts,
    prompt_of,
):
    tok_rows = tokens.shape[0]
    cycle_size = lax.axis_size("ctx")
    device = lax.axis_index("ctx")
    sequence_len = tok_rows * cycle_size
    block_len = tok_rows // 2
    full_tokens = lax.all_gather(tokens, "head", axis=1, tiled=True)

    def add_rows(weight_part):
        return jnp.dot(full_tokens, weight_part, preferred_element_type=jnp.float32)

    frozen_query_output = add_rows(lax.all_gather(query_frozen_matrix, "ctx", axis=0, tiled=True))
    key_base = add_rows(lax.all_gather(key_weight, "ctx", axis=0, tiled=True))
    frozen_value_output = add_rows(lax.all_gather(value_frozen_matrix, "ctx", axis=0, tiled=True))
    own_ids = device * tok_rows + jnp.arange(tok_rows, dtype=jnp.int32)
    own_info = row_meta(own_ids, block_order, doc_starts, prompt_of, block_len, sequence_len)
    local_heads = query_frozen_matrix.shape[1] // HD
    local_kv = key_weight.shape[1] // HD
    per_kv = local_heads // local_kv
    query_adapter_hidden = jnp.dot(
        full_tokens, query_down, preferred_element_type=jnp.float32
    ).astype(jnp.bfloat16)
    query_states = frozen_query_output + adapter_scaling * jnp.dot(
        query_adapter_hidden, query_adapter_expand, preferred_element_type=jnp.float32
    )
    query_states = (
        rotate(query_states.reshape(tok_rows, local_heads, HD), own_info[3]) * query_scale
    ).astype(jnp.bfloat16)
    query_heads = query_states.reshape(tok_rows, local_kv, per_kv, HD)
    key_proj = (
        rotate(key_base.reshape(tok_rows, local_kv, HD), own_info[3])
        .astype(jnp.bfloat16)
        .reshape(tok_rows, local_kv * HD)
    )
    value_adapter_hidden = jnp.dot(
        full_tokens, value_down, preferred_element_type=jnp.float32
    ).astype(jnp.bfloat16)
    value_projected = (
        frozen_value_output
        + adapter_scaling
        * jnp.dot(value_adapter_hidden, value_adapter_expand, preferred_element_type=jnp.float32)
    ).astype(jnp.bfloat16)
    pieces = (
        lax.all_gather(key_proj, "ctx", axis=0, tiled=True),
        lax.all_gather(value_projected, "ctx", axis=0, tiled=True),
    )
    key_ids = jnp.arange(pieces[0].shape[0], dtype=jnp.int32)
    key_block = pieces[0]
    value_block = pieces[1]
    key_info = row_meta(key_ids, block_order, doc_starts, prompt_of, block_len, sequence_len)
    visible = visible_mask(own_info, key_info)
    key_heads = key_block.reshape(key_block.shape[0], local_kv, HD)
    value_heads = value_block.reshape(value_block.shape[0], local_kv, HD)
    scores = jnp.einsum(
        "tkgd,skd->kgts", query_heads, key_heads, preferred_element_type=jnp.float32
    )
    capped = softcap_limit * jnp.tanh(scores / softcap_limit)
    unnorm = jnp.where(visible[None, None], jnp.exp(capped), jnp.zeros_like(capped))
    denominator = jnp.sum(unnorm, axis=-1)
    numerator = jnp.einsum(
        "kgts,skd->tkgd",
        unnorm.astype(jnp.bfloat16),
        value_heads,
        preferred_element_type=jnp.float32,
    )
    numerator, denominator = (numerator, denominator)
    attended = numerator / jnp.transpose(denominator, (2, 0, 1))[..., None]
    return attended.reshape(tok_rows, local_heads * HD).astype(jnp.bfloat16)


def solution(mesh):
    in_specs = (
        P(("tenant", "ctx"), "head"),
        P("ctx", "head"),
        P("ctx", "head"),
        P("ctx", "head"),
        P("tenant", None),
        P("tenant", "head"),
        P("tenant", None),
        P("tenant", "head"),
        P("tenant"),
        P("tenant"),
        P("tenant"),
    )
    out_specs = P(("tenant", "ctx"), "head")
    return jax.shard_map(local, mesh=mesh, in_specs=in_specs, out_specs=out_specs, check_vma=False)
```

profile of v0, /device:TPU:0, one launch (start us, length us, event | category | flops | bytes accessed | tf_op | source)
XLA Modules:
  0.0 143.6 jit_solution(536576771758366168)
XLA Ops:
  6.5 0.0 copy-start
  6.5 0.0 copy-start.1
  6.5 0.0 copy-start.2
  6.5 0.0 copy-start.3
  6.5 0.0 all-gather.9.cloned.1.call-start
  6.6 0.7 all-gather.9.cloned.1.call-update
  7.3 0.0 all-gather.5.cloned.1.call-start
  7.3 0.7 all-gather.5.cloned.1.call-update
  8.0 0.0 all-gather.11.cloned.1.call-start
  8.1 0.7 all-gather.11.cloned.1.call-update
  8.8 0.0 all-gather.7.cloned.1.call-start
  8.8 0.5 all-gather.7.cloned.1.call-update
  9.4 0.0 copy-done.1
  9.4 0.1 slice.15
  9.5 0.0 copy-done.2
  9.5 0.1 select_reduce_fusion.4
  9.6 0.1 convert_reduce_fusion.1
  9.7 0.1 select_reduce_fusion.3
  9.7 0.1 convert_reduce_fusion
  9.8 0.1 add_subtract_fusion
  9.9 0.0 copy-done.3
  9.9 0.1 select_reduce_fusion.1
  10.0 0.1 select_reduce_fusion
  10.1 0.3 multiply_cosine_fusion
  10.4 0.2 and_or_fusion
  10.7 0.0 copy-start.5
  10.7 23.7 %all-gather.9.cloned.1.call-done = bf16[4608,128]{1,0:T(8,128)(2,1)} async-done(((bf16[2304,128]{1,0:T(8,128)(2,1)}), bf16[4608,128]{1,0:T(8,128)(2,1)}) %all-gather.9.cloned.1.call-update) | async-done | bytes 1179664 | tf_op jit(solution)/shard_map/all_gather | solution.py:79
  34.4 33.1 %all-gather.5.cloned.1.call-done = bf16[256,4608]{0,1:T(8,128)(2,1)} async-done(((bf16[256,576]{0,1:T(8,128)(2,1)}), bf16[256,4608]{0,1:T(8,128)(2,1)}) %all-gather.5.cloned.1.call-update) | async-done | bytes 2359312 | tf_op jit(solution)/shard_map/all_gather | solution.py:73
  67.5 0.0 copy-start.4
  67.5 2.7 %fusion.30 = f32[256,128]{0,1:T(8,128)S(1)} fusion(bf16[256,4608]{0,1:T(8,128)(2,1)} %all-gather.5.cloned.1.call-done, bf16[4608,128]{1,0:T(8,128)(2,1)} %all-gather.9.cloned.1.call-done), kind=kOutput, calls=%fused_computation.76 | convolution fusion | flops 301989888 | bytes 3670016 | tf_op jit(solution)/shard_map/dot_general | solution.py:76
  70.4 4.9 %all_gather.22 = bf16[512,128]{0,1:T(8,128)(2,1)S(1)} all-gather(bf16[256,128]{0,1:T(8,128)(2,1)S(1)} %get-tuple-element.13), channel_id=1, replica_groups=mesh['tenant'=2,'ctx'=2,'head'=8] {'ctx'}, dimensions={0}, use_global_device_ids=true | all-gather | bytes 196608 | tf_op jit(solution)/shard_map/all_gather | solution.py:110
  75.3 0.0 copy-done
  75.3 0.0 copy-done.5
  75.3 0.0 copy-done.4
  75.3 1.0 convolution_multiply_fusion.1
  76.3 28.1 %all-gather.11.cloned.1.call-done = bf16[4608,256]{1,0:T(8,128)(2,1)} async-done(((bf16[2304,256]{1,0:T(8,128)(2,1)}), bf16[4608,256]{1,0:T(8,128)(2,1)}) %all-gather.11.cloned.1.call-update) | async-done | bytes 2359312 | tf_op jit(solution)/shard_map/all_gather | solution.py:78
  104.4 2.7 %convolution_add_fusion = f32[256,256]{0,1:T(8,128)S(1)} fusion(f32[256,256]{0,1:T(8,128)S(1)} %convolution_multiply_fusion.1, bf16[256,4608]{0,1:T(8,128)(2,1)S(1)} %copy-done.4, bf16[4608,256]{1,0:T(8,128)(2,1)} %all-gather.11.cloned.1.call-done), kind=kOutput, calls=%fused_computation.7 | convolution fusion | flops 604045312 | bytes 5242880 | tf_op jit(solution)/shard_map/dot_general | solution.py:76
  107.1 2.5 %convolution_multiply_fusion.2 = f32[256,128]{0,1:T(8,128)} fusion(bf16[16,128]{1,0:T(8,128)(2,1)} %param.18, bf16[256,4608]{0,1:T(8,128)(2,1)S(1)} %copy-done.4, bf16[4608,16]{0,1:T(8,128)(2,1)} %param.17), kind=kOutput, calls=%fused_computation.10 | convolution fusion | flops 38834176 | bytes 2641920 | tf_op jit(solution)/shard_map/dot_general | solution.py:107
  109.7 18.9 %all-gather.7.cloned.1.call-done = bf16[4608,128]{1,0:T(8,128)(2,1)} async-done(((bf16[2304,128]{1,0:T(8,128)(2,1)}), bf16[4608,128]{1,0:T(8,128)(2,1)}) %all-gather.7.cloned.1.call-update) | async-done | bytes 1179664 | tf_op jit(solution)/shard_map/all_gather | solution.py:80
  128.6 1.9 %fusion.5 = bf16[256,128]{0,1:T(8,128)(2,1)S(1)} fusion(f32[256,128]{0,1:T(8,128)} %convolution_multiply_fusion.2, bf16[256,4608]{0,1:T(8,128)(2,1)S(1)} %copy-done.4, bf16[4608,128]{1,0:T(8,128)(2,1)} %all-gather.7.cloned.1.call-done), kind=kOutput, calls=%fused_computation.11 | convolution fusion | flops 302055424 | bytes 3735552 | tf_op jit(solution)/shard_map/dot_general | solution.py:76
  130.5 4.9 %all_gather.20 = bf16[512,128]{0,1:T(8,128)(2,1)S(1)} all-gather(bf16[256,128]{0,1:T(8,128)(2,1)S(1)} %fusion.5), channel_id=1, replica_groups=mesh['tenant'=2,'ctx'=2,'head'=8] {'ctx'}, dimensions={0}, use_global_device_ids=true | all-gather | bytes 196608 | tf_op jit(solution)/shard_map/all_gather | solution.py:111
  135.5 0.5 fusion.29
  136.0 0.2 fusion.7
  136.3 0.8 copy.19
  (13 shorter events, 0.2 us)
Async XLA Ops:
  6.5 68.8 %copy-start = (bf16[4608,16]{0,1:T(8,128)(2,1)S(1)}, bf16[4608,16]{0,1:T(8,128)(2,1)}, u32[]{:S(2)}) copy-start(bf16[4608,16]{0,1:T(8,128)(2,1)} %param.15) | copy-start | bytes 442372
  6.5 2.8 %copy-start.1 = (s32[12]{0:T(128)S(1)}, s32[12]{0:T(128)}, u32[]{:S(2)}) copy-start(s32[12]{0:T(128)} %param.20) | copy-start | bytes 148
  6.5 2.9 %copy-start.2 = (s32[4]{0:T(128)S(1)}, s32[4]{0:T(128)}, u32[]{:S(2)}) copy-start(s32[4]{0:T(128)} %param.19) | copy-start | bytes 52
  6.5 3.4 %copy-start.3 = (s32[12]{0:T(128)S(1)}, s32[12]{0:T(128)}, u32[]{:S(2)}) copy-start(s32[12]{0:T(128)} %param.21) | copy-start | bytes 148
  6.5 27.9 %all-gather.9.cloned.1.call-start = ((), (), s32[]{:S(2)}) async-start(), calls=%async_computation.2 | async-start | bytes 1769472 | tf_op jit(solution)/shard_map/all_gather | solution.py:79
  7.3 60.3 %all-gather.5.cloned.1.call-start = ((), (), s32[]{:S(2)}) async-start(), calls=%async_computation | async-start | bytes 2654208 | tf_op jit(solution)/shard_map/all_gather | solution.py:73
  8.0 96.4 %all-gather.11.cloned.1.call-start = ((), (), s32[]{:S(2)}) async-start(), calls=%async_computation.3 | async-start | bytes 3538944 | tf_op jit(solution)/shard_map/all_gather | solution.py:78
  8.8 119.8 %all-gather.7.cloned.1.call-start = ((), (), s32[]{:S(2)}) async-start(), calls=%async_computation.1 | async-start | bytes 1769472 | tf_op jit(solution)/shard_map/all_gather | solution.py:80
  10.7 64.6 %copy-start.5 = (bf16[16,256]{1,0:T(8,128)(2,1)S(1)}, bf16[16,256]{1,0:T(8,128)(2,1)}, u32[]{:S(2)}) copy-start(bf16[16,256]{1,0:T(8,128)(2,1)} %param.16) | copy-start | bytes 24580
  67.5 7.8 %copy-start.4 = (bf16[256,4608]{0,1:T(8,128)(2,1)S(1)}, bf16[256,4608]{0,1:T(8,128)(2,1)}, u32[]{:S(2)}) copy-start(bf16[256,4608]{0,1:T(8,128)(2,1)} %all-gather.5.cloned.1.call-done) | copy-start | bytes 7077892
Sparse Core Ops, SparseCore 0:
  8.9 25.4 all-gather.8
  36.1 31.4 all-gather.4
  69.1 35.2 all-gather.10
  105.8 22.7 all-gather.6
where the time goes:
time: 144 us
  waiting for transfers between devices  106 us (74%)
  between operations  13.3 us (9%)
  matrix products  11.6 us (8%)
  blocking collectives  9.87 us (7%)
    all_gather x1, waiting for transfers between devices, local(): full_tokens = lax.all_gather(tokens, 'head', axis=1, tiled=True)  33.1 us
    all_gather x1, waiting for transfers between devices, local(): lax.all_gather(query_frozen_matrix, 'ctx', axis=0, tiled=True)  28.1 us
    all_gather x1, waiting for transfers between devices, local(): key_base = add_rows(lax.all_gather(key_weight, 'ctx', axis=0, tiled=True))  23.7 us
    all_gather x1, waiting for transfers between devices, local(): lax.all_gather(value_frozen_matrix, 'ctx', axis=0, tiled=True)  18.9 us
    dot_general x3, matrix products, add_rows(): return jnp.dot(full_tokens, weight_part, preferred_element_type=jnp.float32)  7.33 us
    all_gather x1, blocking collectives, local(): lax.all_gather(key_proj, 'ctx', axis=0, tiled=True)  4.93 us
    all_gather x1, blocking collectives, local(): lax.all_gather(value_projected, 'ctx', axis=0, tiled=True)  4.93 us
  transfers between devices with their start and end apart: 4, of which 4 were waited for; matrix products, arithmetic and copies ran while one was open for 7% of the time, Pallas kernels for 0%

commit v1 on v0

--- a/solution.py
+++ b/solution.py
@@ -3,12 +3,29 @@
 import jax.numpy as jnp
 from jax import lax
 from jax.sharding import PartitionSpec as P
+from jax.lax import axis_index, axis_size, ppermute
 
 HD = 128
 softcap_limit = 50.0
 query_scale = 144.0 ** (-0.5)
 adapter_scaling = 2.0
 rope_base = 10000.0
+
+
+def convert_clusters(mat, out_dim=1):
+    full_n = axis_size("head")
+    x_now = map(lambda idx: (idx - 1, idx), range(1, full_n))
+    small = list(x_now)
+    later = small + [(full_n - 1, 0)]
+    plain = mat
+    vals = [plain]
+    for _ in range(full_n - 1):
+        plain = ppermute(plain, "head", later)
+        vals += [plain]
+    parts_out = jnp.concatenate([*reversed(vals)], axis=out_dim)
+    near = axis_index("head")
+    reached = jnp.roll(parts_out, (near + 1) * plain.shape[out_dim], axis=out_dim)
+    return reached
 
 
 def row_meta(row_ids, block_order, doc_starts, prompt_of, block_len, sequence_len):
@@ -70,7 +87,7 @@
     device = lax.axis_index("ctx")
     sequence_len = tok_rows * cycle_size
     block_len = tok_rows // 2
-    full_tokens = lax.all_gather(tokens, "head", axis=1, tiled=True)
+    full_tokens = convert_clusters(tokens)
 
     def add_rows(weight_part):
         return jnp.dot(full_tokens, weight_part, preferred_element_type=jnp.float32)

time: 144 us -> 113 us (0.78)
  waiting for transfers between devices: 106 us -> 51.8 us
  local copies, waits for them, and re-layouts: 0.86 us -> 13.3 us
  other arithmetic: 1.36 us -> 5.3 us
  matrix products: 11.6 us -> 15.4 us
  blocking collectives: 9.87 us -> 13.2 us
    ppermute x0 -> x7, waiting for transfers between devices: none -> 50.2 us  [convert_clusters(): plain = ppermute(plain, 'head', later)]
    all_gather x1 -> x0, waiting for transfers between devices: 33.1 us -> none  [local(): full_tokens = lax.all_gather(tokens, 'head', axis=1, tiled=True)]
    all_gather x1, waiting for transfers between devices: 28.1 us -> 0.02 us  [local(): lax.all_gather(query_frozen_matrix, 'ctx', axis=0, tiled=True)]
    all_gather x1, waiting for transfers between devices: 23.7 us -> 0.01 us  [local(): key_base = add_rows(lax.all_gather(key_weight, 'ctx', axis=0, tiled=True))]
    all_gather x1, waiting for transfers between devices: 18.9 us -> 0.02 us  [local(): lax.all_gather(value_frozen_matrix, 'ctx', axis=0, tiled=True)]
    unnamed x12 -> x25, local copies, waits for them, and re-layouts: 0.03 us -> 11.1 us
    dot_general x3, matrix products: 7.33 us -> 9.36 us  [add_rows(): return jnp.dot(full_tokens, weight_part, preferred_element_type=jnp.float32)]
    all_gather x1, blocking collectives: 4.93 us -> 6.7 us  [local(): lax.all_gather(value_projected, 'ctx', axis=0, tiled=True)]
  transfers between devices with their start and end apart: 4 -> 10, of which waited for: 4 -> 7; matrix products, arithmetic and copies ran while one was open for 7% -> 25% of each run, Pallas kernels for 0% -> 0%
where the time goes in v1:
time: 113 us
  waiting for transfers between devices  51.8 us (46%)
  matrix products  15.4 us (14%)
  local copies, waits for them, and re-layouts  13.3 us (12%)
  between operations  13.3 us (12%)
  blocking collectives  13.2 us (12%)
  other arithmetic  5.3 us (5%)
    ppermute x7, waiting for transfers between devices, convert_clusters(): plain = ppermute(plain, 'head', later)  50.2 us
    unnamed x25, local copies, waits for them, and re-layouts  11.1 us
    dot_general x3, matrix products, add_rows(): return jnp.dot(full_tokens, weight_part, preferred_element_type=jnp.float32)  9.36 us
    all_gather x1, blocking collectives, local(): lax.all_gather(value_projected, 'ctx', axis=0, tiled=True)  6.7 us
    all_gather x1, blocking collectives, local(): lax.all_gather(key_proj, 'ctx', axis=0, tiled=True)  6.49 us
    dot_general x1, matrix products, local(): jnp.dot(query_adapter_hidden, query_adapter_expand, preferred_element_typ...  2.67 us
    dot_general x1, matrix products, local(): jnp.dot(value_adapter_hidden, value_adapter_expand, preferred_element_typ...  2.63 us
  transfers between devices with their start and end apart: 10, of which 7 were waited for; matrix products, arithmetic and copies ran while one was open for 25% of the time, Pallas kernels for 0%

profile of v1, /device:TPU:0, one launch (start us, length us, event | category | flops | bytes accessed | tf_op | source)
XLA Modules:
  0.0 112.9 jit_solution(1882307261535063923)
XLA Ops:
  6.5 0.0 copy-start
  6.5 0.0 all-gather.4.cloned.1.call-start
  6.5 0.7 all-gather.4.cloned.1.call-update
  7.3 0.0 all-gather.6.cloned.1.call-start
  7.3 0.7 all-gather.6.cloned.1.call-update
  8.0 0.0 all-gather.8.cloned.1.call-start
  8.1 0.5 collective-permute-start
  8.6 0.1 all-gather.8.cloned.1.call-update
  8.8 0.7 slice.15
  9.5 0.7 select_reduce_fusion.4
  10.3 0.7 convert_reduce_fusion.1
  11.0 6.2 %collective-permute-done = bf16[256,576]{0,1:T(8,128)(2,1)S(1)} collective-permute-done((bf16[256,576]{0,1:T(8,128)(2,1)}, bf16[256,576]{0,1:T(8,128)(2,1)S(1)}, u32[]{:S(2)}, u32[]{:S(2)}) %collective-permute-start) | collective-permute-done | bytes 294944 | tf_op jit(solution)/shard_map/ppermute | solution.py:23
  17.2 0.0 collective-permute-start.1
  17.3 0.8 select_reduce_fusion.1
  18.0 7.2 %collective-permute-done.1 = bf16[256,576]{0,1:T(8,128)(2,1)S(1)} collective-permute-done((bf16[256,576]{0,1:T(8,128)(2,1)S(1)}, bf16[256,576]{0,1:T(8,128)(2,1)S(1)}, u32[]{:S(2)}, u32[]{:S(2)}) %collective-permute-start.1) | collective-permute-done | bytes 294944 | tf_op jit(solution)/shard_map/ppermute | solution.py:23
  25.2 0.0 collective-permute-start.2
  25.2 0.7 select_reduce_fusion.3
  25.9 7.2 %collective-permute-done.2 = bf16[256,576]{0,1:T(8,128)(2,1)S(1)} collective-permute-done((bf16[256,576]{0,1:T(8,128)(2,1)S(1)}, bf16[256,576]{0,1:T(8,128)(2,1)S(1)}, u32[]{:S(2)}, u32[]{:S(2)}) %collective-permute-start.2) | collective-permute-done | bytes 294944 | tf_op jit(solution)/shard_map/ppermute | solution.py:23
  33.1 0.0 collective-permute-start.3
  33.1 0.7 convert_reduce_fusion
  33.9 0.7 add_subtract_fusion
  34.6 6.5 %collective-permute-done.3 = bf16[256,576]{0,1:T(8,128)(2,1)S(1)} collective-permute-done((bf16[256,576]{0,1:T(8,128)(2,1)S(1)}, bf16[256,576]{0,1:T(8,128)(2,1)S(1)}, u32[]{:S(2)}, u32[]{:S(2)}) %collective-permute-start.3) | collective-permute-done | bytes 294944 | tf_op jit(solution)/shard_map/ppermute | solution.py:23
  41.1 0.0 collective-permute-start.4
  41.1 0.1 select_reduce_fusion
  41.2 7.8 %collective-permute-done.4 = bf16[256,576]{0,1:T(8,128)(2,1)S(1)} collective-permute-done((bf16[256,576]{0,1:T(8,128)(2,1)S(1)}, bf16[256,576]{0,1:T(8,128)(2,1)S(1)}, u32[]{:S(2)}, u32[]{:S(2)}) %collective-permute-start.4) | collective-permute-done | bytes 294944 | tf_op jit(solution)/shard_map/ppermute | solution.py:23
  49.0 0.0 collective-permute-start.5
  49.0 0.3 multiply_cosine_fusion
  49.4 7.6 %collective-permute-done.5 = bf16[256,576]{0,1:T(8,128)(2,1)S(1)} collective-permute-done((bf16[256,576]{0,1:T(8,128)(2,1)S(1)}, bf16[256,576]{0,1:T(8,128)(2,1)S(1)}, u32[]{:S(2)}, u32[]{:S(2)}) %collective-permute-start.5) | collective-permute-done | bytes 294944 | tf_op jit(solution)/shard_map/ppermute | solution.py:23
  57.0 0.0 collective-permute-start.6
  57.0 0.2 and_or_fusion
  57.2 0.0 copy-start.2
  57.2 0.0 copy-start.4
  57.3 7.7 %collective-permute-done.6 = bf16[256,576]{0,1:T(8,128)(2,1)S(1)} collective-permute-done((bf16[256,576]{0,1:T(8,128)(2,1)S(1)}, bf16[256,576]{0,1:T(8,128)(2,1)S(1)}, u32[]{:S(2)}, u32[]{:S(2)}) %collective-permute-start.6) | collective-permute-done | bytes 294944 | tf_op jit(solution)/shard_map/ppermute | solution.py:23
  64.9 0.7 constant_dynamic-update-slice_fusion.15
  65.7 0.7 constant_dynamic-update-slice_fusion.14
  66.4 0.7 constant_dynamic-update-slice_fusion.13
  67.1 0.7 constant_dynamic-update-slice_fusion.12
  67.9 0.7 constant_dynamic-update-slice_fusion.11
  68.6 0.7 constant_dynamic-update-slice_fusion.10
  69.3 0.7 constant_dynamic-update-slice_fusion.9
  70.1 0.8 constant_dynamic-update-slice_fusion.8
  70.8 0.7 constant_dynamic-update-slice_fusion.7
  71.6 0.7 constant_dynamic-update-slice_fusion.6
  72.3 0.7 constant_dynamic-update-slice_fusion.5
  73.0 0.7 constant_dynamic-update-slice_fusion.4
  73.8 0.7 constant_dynamic-update-slice_fusion.3
  74.5 0.8 constant_dynamic-update-slice_fusion.2
  75.3 0.7 constant_dynamic-update-slice_fusion.1
  76.0 0.8 constant_dynamic-update-slice_fusion
  76.7 0.0 copy-done.2
  76.8 2.6 %convolution_multiply_fusion.2 = f32[256,128]{0,1:T(8,128)S(1)} fusion(bf16[16,128]{1,0:T(8,128)(2,1)S(1)} %copy-done.4, bf16[4608,16]{0,1:T(8,128)(2,1)S(1)} %copy-done.2, bf16[256,9216]{0,1:T(8,128)(2,1)} %constant_dynamic-update-slice_fusion, s32[]{:T(128)S(6)} %select_n.89), kind=kOutput, calls=%fused_computation.20 | convolution fusion | flops 38834176 | bytes 2641924 | tf_op jit(solution)/shard_map/dot_general | solution.py:124
  79.4 0.0 copy-start.3
  79.4 0.0 all-gather.4.cloned.1.call-done
  79.4 2.9 %fusion.21 = bf16[256,128]{0,1:T(8,128)(2,1)S(1)} fusion(f32[256,128]{0,1:T(8,128)S(1)} %convolution_multiply_fusion.2, bf16[4608,128]{1,0:T(8,128)(2,1)} %all-gather.4.cloned.1.call-done, bf16[256,9216]{0,1:T(8,128)(2,1)} %constant_dynamic-update-slice_fusion, s32[]{:T(128)S(6)} %select_n.89), kind=kOutput, calls=%fused_computation.21 | convolution fusion | flops 302055424 | bytes 3735556 | tf_op jit(solution)/shard_map/dot_general | solution.py:93
  82.3 6.7 %all_gather.16 = bf16[512,128]{0,1:T(8,128)(2,1)S(1)} all-gather(bf16[256,128]{0,1:T(8,128)(2,1)S(1)} %fusion.21), channel_id=1, replica_groups=mesh['tenant'=2,'ctx'=2,'head'=8] {'ctx'}, dimensions={0}, use_global_device_ids=true | all-gather | bytes 196608 | tf_op jit(solution)/shard_map/all_gather | solution.py:128
  89.0 2.9 %fusion.9 = f32[256,128]{0,1:T(8,128)S(1)} fusion(bf16[4608,128]{1,0:T(8,128)(2,1)} %all-gather.6.cloned.1.call-done, bf16[256,9216]{0,1:T(8,128)(2,1)} %constant_dynamic-update-slice_fusion, s32[]{:T(128)S(6)} %select_n.89), kind=kOutput, calls=%fused_computation.10 | convolution fusion | flops 301989888 | bytes 3670020 | tf_op jit(solution)/shard_map/dot_general | solution.py:93
  91.9 6.5 %all_gather.18 = bf16[512,128]{0,1:T(8,128)(2,1)S(1)} all-gather(bf16[256,128]{0,1:T(8,128)(2,1)S(1)} %get-tuple-element.13), channel_id=1, replica_groups=mesh['tenant'=2,'ctx'=2,'head'=8] {'ctx'}, dimensions={0}, use_global_device_ids=true | all-gather | bytes 196608 | tf_op jit(solution)/shard_map/all_gather | solution.py:127
  98.4 0.0 copy-done.3
  98.4 2.7 %convolution_multiply_fusion.1 = f32[256,256]{0,1:T(8,128)S(1)} fusion(bf16[16,256]{1,0:T(8,128)(2,1)S(1)} %copy-done.3, bf16[4608,16]{0,1:T(8,128)(2,1)S(1)} %copy-done, bf16[256,9216]{0,1:T(8,128)(2,1)} %constant_dynamic-update-slice_fusion, s32[]{:T(128)S(6)} %select_n.89), kind=kOutput, calls=%fused_computation.18 | convolution fusion | flops 39915520 | bytes 2777092 | tf_op jit(solution)/shard_map/dot_general | solution.py:106
  101.1 0.0 all-gather.8.cloned.1.call-done
  101.1 3.6 %fusion.15 = f32[256,256]{0,1:T(8,128)S(1)} fusion(f32[256,256]{0,1:T(8,128)S(1)} %convolution_multiply_fusion.1, bf16[4608,256]{1,0:T(8,128)(2,1)} %all-gather.8.cloned.1.call-done, bf16[256,9216]{0,1:T(8,128)(2,1)} %constant_dynamic-update-slice_fusion, s32[]{:T(128)S(6)} %select_n.89), kind=kOutput, calls=%fused_computation.16 | convolution fusion | flops 604045312 | bytes 5242884 | tf_op jit(solution)/shard_map/dot_general | solution.py:93
  104.9 0.5 fusion.64
  105.4 0.2 fusion.35
  105.6 0.8 copy.19
  (18 shorter events, 0.2 us)
Async XLA Ops:
  6.5 91.9 %copy-start = (bf16[4608,16]{0,1:T(8,128)(2,1)S(1)}, bf16[4608,16]{0,1:T(8,128)(2,1)}, u32[]{:S(2)}) copy-start(bf16[4608,16]{0,1:T(8,128)(2,1)} %param.15) | copy-start | bytes 442372
  6.5 63.5 %copy-start.1 = (bf16[256,576]{0,1:T(8,128)(2,1)S(1)}, bf16[256,576]{0,1:T(8,128)(2,1)}, u32[]{:S(2)}) copy-start(bf16[256,576]{0,1:T(8,128)(2,1)} %param.11) | copy-start | bytes 884740
  6.5 72.9 %all-gather.4.cloned.1.call-start = ((), (), s32[]{:S(2)}) async-start(), calls=%async_computation | async-start | bytes 1769472 | tf_op jit(solution)/shard_map/all_gather | solution.py:97
  7.3 81.8 %all-gather.6.cloned.1.call-start = ((), (), s32[]{:S(2)}) async-start(), calls=%async_computation.1 | async-start | bytes 1769472 | tf_op jit(solution)/shard_map/all_gather | solution.py:96
  8.0 93.1 %all-gather.8.cloned.1.call-start = ((), (), s32[]{:S(2)}) async-start(), calls=%async_computation.2 | async-start | bytes 3538944 | tf_op jit(solution)/shard_map/all_gather | solution.py:95
  8.1 9.2 %collective-permute-start = (bf16[256,576]{0,1:T(8,128)(2,1)}, bf16[256,576]{0,1:T(8,128)(2,1)S(1)}, u32[]{:S(2)}, u32[]{:S(2)}) collective-permute-start(bf16[256,576]{0,1:T(8,128)(2,1)} %param.11), channel_id=1, source_target_pairs={{0,1},{1,2},{2,3},{3,4},{4,5},{5,6},{6,7},{7,0},{8,9},{9,10},{10,1... | collective-permute-start | bytes 884744 | tf_op jit(solution)/shard_map/ppermute | solution.py:23
  17.2 7.9 %collective-permute-start.1 = (bf16[256,576]{0,1:T(8,128)(2,1)S(1)}, bf16[256,576]{0,1:T(8,128)(2,1)S(1)}, u32[]{:S(2)}, u32[]{:S(2)}) collective-permute-start(bf16[256,576]{0,1:T(8,128)(2,1)S(1)} %collective-permute-done), channel_id=1, source_target_pairs={{0,1},{1,2},{2,3},{3,4},{4,5},{5,6},{6,7},{7,0},{8,9},{9,10},{10,1... | collective-permute-start | bytes 884744 | tf_op jit(solution)/shard_map/ppermute | solution.py:23
  25.2 7.9 %collective-permute-start.2 = (bf16[256,576]{0,1:T(8,128)(2,1)S(1)}, bf16[256,576]{0,1:T(8,128)(2,1)S(1)}, u32[]{:S(2)}, u32[]{:S(2)}) collective-permute-start(bf16[256,576]{0,1:T(8,128)(2,1)S(1)} %collective-permute-done.1), channel_id=1, source_target_pairs={{0,1},{1,2},{2,3},{3,4},{4,5},{5,6},{6,7},{7,0},{8,9},{9,10},{10,1... | collective-permute-start | bytes 884744 | tf_op jit(solution)/shard_map/ppermute | solution.py:23
  33.1 7.9 %collective-permute-start.3 = (bf16[256,576]{0,1:T(8,128)(2,1)S(1)}, bf16[256,576]{0,1:T(8,128)(2,1)S(1)}, u32[]{:S(2)}, u32[]{:S(2)}) collective-permute-start(bf16[256,576]{0,1:T(8,128)(2,1)S(1)} %collective-permute-done.2), channel_id=1, source_target_pairs={{0,1},{1,2},{2,3},{3,4},{4,5},{5,6},{6,7},{7,0},{8,9},{9,10},{10,1... | collective-permute-start | bytes 884744 | tf_op jit(solution)/shard_map/ppermute | solution.py:23
  41.1 7.9 %collective-permute-start.4 = (bf16[256,576]{0,1:T(8,128)(2,1)S(1)}, bf16[256,576]{0,1:T(8,128)(2,1)S(1)}, u32[]{:S(2)}, u32[]{:S(2)}) collective-permute-start(bf16[256,576]{0,1:T(8,128)(2,1)S(1)} %collective-permute-done.3), channel_id=1, source_target_pairs={{0,1},{1,2},{2,3},{3,4},{4,5},{5,6},{6,7},{7,0},{8,9},{9,10},{10,1... | collective-permute-start | bytes 884744 | tf_op jit(solution)/shard_map/ppermute | solution.py:23
  49.0 7.9 %collective-permute-start.5 = (bf16[256,576]{0,1:T(8,128)(2,1)S(1)}, bf16[256,576]{0,1:T(8,128)(2,1)S(1)}, u32[]{:S(2)}, u32[]{:S(2)}) collective-permute-start(bf16[256,576]{0,1:T(8,128)(2,1)S(1)} %collective-permute-done.4), channel_id=1, source_target_pairs={{0,1},{1,2},{2,3},{3,4},{4,5},{5,6},{6,7},{7,0},{8,9},{9,10},{10,1... | collective-permute-start | bytes 884744 | tf_op jit(solution)/shard_map/ppermute | solution.py:23
  57.0 7.9 %collective-permute-start.6 = (bf16[256,576]{0,1:T(8,128)(2,1)S(1)}, bf16[256,576]{0,1:T(8,128)(2,1)S(1)}, u32[]{:S(2)}, u32[]{:S(2)}) collective-permute-start(bf16[256,576]{0,1:T(8,128)(2,1)S(1)} %collective-permute-done.5), channel_id=1, source_target_pairs={{0,1},{1,2},{2,3},{3,4},{4,5},{5,6},{6,7},{7,0},{8,9},{9,10},{10,1... | collective-permute-start | bytes 884744 | tf_op jit(solution)/shard_map/ppermute | solution.py:23
  57.2 19.5 %copy-start.2 = (bf16[4608,16]{0,1:T(8,128)(2,1)S(1)}, bf16[4608,16]{0,1:T(8,128)(2,1)}, u32[]{:S(2)}) copy-start(bf16[4608,16]{0,1:T(8,128)(2,1)} %param.17) | copy-start | bytes 442372
  57.2 19.5 %copy-start.4 = (bf16[16,128]{1,0:T(8,128)(2,1)S(1)}, bf16[16,128]{1,0:T(8,128)(2,1)}, u32[]{:S(2)}) copy-start(bf16[16,128]{1,0:T(8,128)(2,1)} %param.18) | copy-start | bytes 12292
  79.4 19.1 %copy-start.3 = (bf16[16,256]{1,0:T(8,128)(2,1)S(1)}, bf16[16,256]{1,0:T(8,128)(2,1)}, u32[]{:S(2)}) copy-start(bf16[16,256]{1,0:T(8,128)(2,1)} %param.16) | copy-start | bytes 24580
Sparse Core Ops, SparseCore 0:
  8.9 25.4 all-gather.3
  35.9 22.7 all-gather.5
  60.3 38.8 all-gather.7
